TPU v7x, 32 devices: a whole 2x2x4 slice. The times are simulated.
32 devices in a mesh: seq: 8 (over z, y), batch: 4 (over x, core).
Axes of the slice: x: 2, y: 2, z: 4, core: 2. Of those that a mesh axis runs over, the one named last changes fastest.
Arguments:
- tokens: bfloat16 [4096, 1440], P(('batch', 'seq')), parts along dimension 0, may hold values from -6 to 6
- norm_gain: float32 [1440], replicated, may hold values from 0.1 to 1.9
- qkv_weight: bfloat16 [1440, 2560], P(None, 'seq'), may hold values from -2 to 2
- sinks: float32 [32], replicated, may hold values from 0 to 5
- out_weight: bfloat16 [2048, 1440], P('seq'), may hold values from -0.125 to 0.125
- moe_gain: float32 [1440], replicated, may hold values from 0.1 to 1.9
- expert_in: bfloat16 [8, 1440, 2880], P('seq'), may hold values from -0.15625 to 0.15625
- expert_out: bfloat16 [8, 1440, 1440], P('seq'), may hold values from -0.15625 to 0.15625
- expert_ids: int32 [4096, 4], P(('batch', 'seq')), parts along dimension 0, may hold values from 0 to 7, all different within a row; in each aligned block of 128 rows (0 to 127, 128 to 255, ...) at most 128 rows name the same one
- gate_ints: int32 [4096, 4], P(('batch', 'seq')), parts along dimension 0, may hold values from 1 to 4096
Outputs:
- block_out: bfloat16 [4096, 1440], P(('batch', 'seq')), parts along dimension 0
There are 4 independent parts, one for each index of `batch`. A program takes and returns all parts, laid end to end along the dimension named above; an argument that names none is the same for every part. Nothing has to cross between parts.
Inputs may be any that keep to these rules, and one draw needn't show every extreme that they name: `expert_ids`: each row names 4 different experts; among the 128 rows of one device no expert is named more than 128 times.
All inputs are finite; a program needn't handle non-finite values.
Results may differ from a plain program's by a relative error of at most 0.012.
Values may be sent and summed in bfloat16 or wider, within the bound.
A program may use at most 128 MiB of HBM per device.

v0:
```python
import math

import jax
import jax.numpy as jnp
from jax import lax
from jax.sharding import PartitionSpec as P

QH = 32
KVH = 4
HD = 64
WIN = 128
TOP = 4


epsilon = 1e-05
rope_base = 150000.0
glu_slope = 1.702


def shifted(value, axis, steps):
    count = lax.axis_size(axis)
    initial, last = (max(0, -steps), min(count, count - steps))
    return lax.ppermute(value, axis, [(source, source + steps) for source in range(initial, last)])


def norm_scale(values, gain):
    widened = values.astype(jnp.float32)
    mean_sq = jnp.mean(widened * widened, axis=-1, keepdims=True)
    return widened * lax.rsqrt(mean_sq + epsilon) * gain


def rotate(values, positions):
    half_width = values.shape[-1] // 2
    freq_steps = jnp.arange(half_width).astype(jnp.float32)
    inverse = jnp.exp(freq_steps * (-2.0 * math.log(rope_base) / values.shape[-1]))
    angles = positions[:, None] * inverse[None, :]
    cosine = jnp.cos(angles)[:, None, :]
    sine_term = jnp.sin(angles)[:, None, :]
    lower_half = values[..., :half_width]
    second = values[..., half_width:]
    return jnp.concatenate(
        [lower_half * cosine - second * sine_term, second * cosine + lower_half * sine_term],
        axis=-1,
    )


def band_block(queries, key_heads, value_heads, sinks, first_pos):
    count = queries.shape[0]
    groups = QH // KVH
    grouped = queries.reshape(count, KVH, groups, HD)
    scores = jnp.einsum(
        "tkgd,skd->kgts", grouped, key_heads, preferred_element_type=jnp.float32
    ) * (1.0 / math.sqrt(HD))
    query_pos = first_pos + jnp.arange(count)
    key_pos = first_pos - count + jnp.arange(2 * count)
    distance = query_pos[:, None] - key_pos[None, :]
    allowed = (distance >= 0) & (distance < WIN) & (key_pos >= 0)[None, :]
    scores = jnp.where(allowed[None, None, :, :], scores, -jnp.inf)
    sink_logit = sinks.reshape(KVH, groups, 1, 1)
    row_peak = jnp.maximum(jnp.max(scores, axis=-1, keepdims=True), sink_logit)
    raised = jnp.exp(scores - row_peak)
    totals = jnp.sum(raised, axis=-1, keepdims=True) + jnp.exp(sink_logit - row_peak)
    weights = (raised / totals).astype(jnp.bfloat16)
    mixture = jnp.einsum("kgts,skd->tkgd", weights, value_heads, preferred_element_type=jnp.float32)
    return mixture.reshape(count, QH * HD).astype(jnp.bfloat16)


def run_expert(incoming, weight_in, weight_out):
    width = incoming.shape[-1]
    hidden_width = weight_in.shape[1] // 2
    flat_rows = incoming.reshape(-1, width)
    paired = jnp.dot(flat_rows, weight_in, preferred_element_type=jnp.float32)
    gate_part = paired[:, :hidden_width]
    up_part = paired[:, hidden_width:]
    activated = (gate_part * jax.nn.sigmoid(glu_slope * gate_part) * (up_part + 1.0)).astype(
        jnp.bfloat16
    )
    produced = jnp.dot(activated, weight_out, preferred_element_type=jnp.float32).astype(
        jnp.bfloat16
    )
    return produced.reshape(incoming.shape)


def local(
    tokens,
    norm_gain,
    qkv_weight,
    sinks,
    out_weight,
    moe_gain,
    expert_in,
    expert_out,
    expert_ids,
    gate_ints,
):
    local_rows = tokens.shape[0]
    width = tokens.shape[1]
    devices = lax.axis_size("seq")
    device_index = lax.axis_index("seq")
    capacity = 2 * local_rows * TOP // devices
    query_cols = QH * HD
    key_cols = KVH * HD
    residual = tokens.astype(jnp.float32)
    normed = norm_scale(tokens, norm_gain).astype(jnp.bfloat16)
    spread = jnp.dot(
        lax.all_gather(normed, "seq", axis=0, tiled=True),
        qkv_weight,
        preferred_element_type=jnp.float32,
    )
    projections = lax.all_to_all(spread, "seq", split_axis=0, concat_axis=1, tiled=True)
    first_pos = device_index * local_rows
    positions = (first_pos + jnp.arange(local_rows)).astype(jnp.float32)
    queries = rotate(projections[:, :query_cols].reshape(local_rows, QH, HD), positions).astype(
        jnp.bfloat16
    )
    key_heads = rotate(
        projections[:, query_cols : query_cols + key_cols].reshape(local_rows, KVH, HD), positions
    ).astype(jnp.bfloat16)
    value_heads = (
        projections[:, query_cols + key_cols :].reshape(local_rows, KVH, HD).astype(jnp.bfloat16)
    )
    prev_keys, prev_values = shifted((key_heads, value_heads), "seq", 1)
    key_block = jnp.concatenate([prev_keys, key_heads], axis=0)
    value_block = jnp.concatenate([prev_values, value_heads], axis=0)
    attention = band_block(queries, key_block, value_block, sinks, first_pos)
    projected = jnp.dot(
        attention,
        lax.all_gather(out_weight, "seq", axis=0, tiled=True),
        preferred_element_type=jnp.float32,
    )
    residual_mid = (residual + projected).astype(jnp.bfloat16)
    moe_input = norm_scale(residual_mid, moe_gain).astype(jnp.bfloat16)
    flat_ids = expert_ids.reshape(-1)
    onehot = (flat_ids[:, None] == jnp.arange(devices)[None, :]).astype(jnp.int32)
    before = jnp.cumsum(onehot, axis=0) - onehot
    slot_index = jnp.sum(before * onehot, axis=1)
    target = flat_ids * capacity + slot_index
    matches = target[None, :] == jnp.arange(devices * capacity)[:, None]
    owner_row = jnp.sum(jnp.where(matches, jnp.arange(local_rows * TOP)[None, :], 0), axis=1)
    filled = jnp.any(matches, axis=1)
    gathered = jnp.take(moe_input, owner_row // TOP, axis=0)
    outgoing = jnp.where(filled[:, None], gathered, jnp.zeros_like(gathered)).reshape(
        devices, capacity, width
    )
    arrived = lax.all_to_all(outgoing, "seq", split_axis=0, concat_axis=0, tiled=True)
    returned = lax.all_to_all(
        run_expert(arrived, expert_in[0], expert_out[0]),
        "seq",
        split_axis=0,
        concat_axis=0,
        tiled=True,
    )
    picked = jnp.take(returned.reshape(-1, width), target, axis=0).reshape(local_rows, TOP, width)
    route_weight = gate_ints.astype(jnp.float32)
    route_weight = route_weight / jnp.sum(route_weight, axis=-1, keepdims=True)
    combined = residual_mid.astype(jnp.float32)
    for which in range(TOP):
        combined = combined + route_weight[:, which : which + 1] * picked[:, which].astype(
            jnp.float32
        )
    return combined.astype(jnp.bfloat16)


def solution(mesh):
    return jax.shard_map(
        local,
        mesh=mesh,
        in_specs=(
            P(("batch", "seq"), None),
            P(),
            P(None, "seq"),
            P(),
            P("seq", None),
            P(),
            P("seq", None, None),
            P("seq", None, None),
            P(("batch", "seq"), None),
            P(("batch", "seq"), None),
        ),
        out_specs=P(("batch", "seq"), None),
        check_vma=False,
    )
```

profile of v0, /device:TPU:0, one launch (start us, length us, event | category | flops | bytes accessed | tf_op | source)
XLA Modules:
  0.0 396.1 jit_solution(2990338177495077095)
XLA Ops:
  6.5 1.3 fusion.24
  7.8 2.0 fusion.26
  10.6 0.8 copy.60
  12.4 1.1 reduce-window.6
  13.7 59.4 %all-gather.3.cloned.1.call-done = bf16[1024,1440]{0,1:T(8,128)(2,1)} async-done(((bf16[128,1440]{0,1:T(8,128)(2,1)}), bf16[1024,1440]{0,1:T(8,128)(2,1)}) %all-gather.3.cloned.1.call-update) | async-done | bytes 2949136 | tf_op jit(solution)/shard_map/all_gather | solution.py:106
  73.1 3.0 convolution_bitcast_fusion
  76.1 1.2 copy.83
  77.3 3.6 all-to-all-start
  82.0 53.5 %all-to-all-done = f32[8,128,320]{1,2,0:T(8,128)S(1)} async-done(((f32[8,128,320]{1,2,0:T(8,128)}), f32[8,128,320]{1,2,0:T(8,128)S(1)}, u32[]{:S(2)}, u32[]{:S(2)}) %all-to-all-start) | async-done | bytes 1310752 | tf_op jit(solution)/shard_map/all_to_all | solution.py:110
  135.6 3.3 collective-permute-start.1
  139.1 1.9 collective-permute-start
  141.0 1.6 collective-permute-done.1
  143.4 0.9 fusion.9
  144.7 1.2 fusion.23
  145.9 46.5 %all-gather.5.cloned.1.call-done = bf16[2048,1440]{0,1:T(8,128)(2,1)} async-done(((bf16[256,1440]{0,1:T(8,128)(2,1)}), bf16[2048,1440]{0,1:T(8,128)(2,1)}) %all-gather.5.cloned.1.call-update) | async-done | bytes 5898256 | tf_op jit(solution)/shard_map/all_gather | solution.py:128
  192.4 4.5 %multiply_reduce_fusion = (f32[128]{0:T(128)S(1)}, f32[128,1440]{0,1:T(8,128)S(1)}) fusion(bf16[2048,1440]{0,1:T(8,128)(2,1)} %all-gather.5.cloned.1.call-done, bf16[128,2048]{0,1:T(8,128)(2,1)S(1)} %bitcast.144, bf16[128,1440]{0,1:T(8,128)(2,1)S(1)} %copy-done.4), kind=kOutput, calls=%fused_computation.46 | convolution fusion | flops 756080512 | bytes 7528960 | tf_op jit(solution)/shard_map/dot_general | solution.py:126
  196.9 0.9 copy-done.2
  198.2 4.2 %gather_fusion = bf16[1024,1440]{1,0:T(8,128)(2,1)S(1)} fusion(bf16[128,1440]{1,0:T(8,128)(2,1)S(1)} %copy.63, s32[1024]{0:T(1024)S(1)} %broadcast_clamp_fusion), kind=kCustom, calls=%fused_computation | custom fusion | bytes 5902336 | tf_op jit(solution)/shard_map/jit(_take)/gather | solution.py:141
  202.4 2.8 copy.64
  205.2 2.2 select_select_fusion
  207.3 71.3 %all_to_all.29 = bf16[8,128,1440]{1,2,0:T(8,128)(2,1)S(1)} all-to-all(bf16[8,128,1440]{1,2,0:T(8,128)(2,1)S(1)} %select_select_fusion), channel_id=1, replica_groups=mesh['seq'=8,'batch'=4] {'seq'}, dimensions={0} | all-to-all | bytes 5898240 | tf_op jit(solution)/shard_map/all_to_all | solution.py:145
  278.6 15.0 %fusion = f32[1024,2880]{0,1:T(8,128)} fusion(bf16[1,1440,2880]{2,1,0:T(8,128)(2,1)} %param.16, bf16[8,128,1440]{1,2,0:T(8,128)(2,1)S(1)} %all_to_all.29), kind=kOutput, calls=%fused_computation.2 | convolution fusion | flops 8493465600 | bytes 23040000 | tf_op jit(solution)/shard_map/dot_general | solution.py:72
  293.6 9.4 %fusion.18 = bf16[180,8,8,128]{3,2,1,0:T(8,128)(2,1)S(1)} fusion(bf16[1,1440,1440]{2,1,0:T(8,128)(2,1)S(1)} %bitcast.143, f32[1024,2880]{0,1:T(8,128)} %fusion), kind=kOutput, calls=%fused_computation.26 | convolution fusion | flops 4260003840 | bytes 18892800 | tf_op jit(solution)/shard_map/dot_general | solution.py:78
  303.0 2.1 copy.82
  305.1 4.8 %all-to-all-start.2 = ((bf16[8,128,1440]{1,2,0:T(8,128)(2,1)}), bf16[8,128,1440]{1,2,0:T(8,128)(2,1)}, u32[]{:S(2)}, u32[]{:S(2)}) async-start(bf16[8,128,1440]{1,2,0:T(8,128)(2,1)} %bitcast.124), calls=%async_computation.2 | async-start | bytes 5898240 | tf_op jit(solution)/shard_map/all_to_all | solution.py:146
  310.4 64.8 %all-to-all-done.2 = bf16[8,128,1440]{1,2,0:T(8,128)(2,1)} async-done(((bf16[8,128,1440]{1,2,0:T(8,128)(2,1)}), bf16[8,128,1440]{1,2,0:T(8,128)(2,1)}, u32[]{:S(2)}, u32[]{:S(2)}) %all-to-all-start.2) | async-done | bytes 2949152 | tf_op jit(solution)/shard_map/all_to_all | solution.py:146
  375.2 3.1 copy.67
  378.3 3.0 gather_fusion.1
  381.3 2.9 gather.15
  384.2 2.4 copy.69
  386.7 1.5 broadcast_select_fusion
  388.2 1.1 fusion.28
  (70 shorter events, 5.4 us)
Async XLA Ops:
  6.5 66.6 %copy-start = (bf16[1440,320]{0,1:T(8,128)(2,1)S(1)}, bf16[1440,320]{0,1:T(8,128)(2,1)}, u32[]{:S(2)}) copy-start(bf16[1440,320]{0,1:T(8,128)(2,1)} %param.12) | copy-start | bytes 2764804
  6.5 66.6 %all-gather.3.cloned.1.call-start = ((), (), s32[]{:S(2)}) async-start(), calls=%async_computation.3 | async-start | bytes 3317760 | tf_op jit(solution)/shard_map/all_gather | solution.py:106
  9.8 182.6 %all-gather.5.cloned.1.call-start = ((), (), s32[]{:S(2)}) async-start(), calls=%async_computation.4 | async-start | bytes 6635520 | tf_op jit(solution)/shard_map/all_gather | solution.py:128
  77.3 58.1 %all-to-all-start = ((f32[8,128,320]{1,2,0:T(8,128)}), f32[8,128,320]{1,2,0:T(8,128)S(1)}, u32[]{:S(2)}, u32[]{:S(2)}) async-start(f32[8,128,320]{1,2,0:T(8,128)} %bitcast.125), calls=%async_computation | async-start | bytes 2621440 | tf_op jit(solution)/shard_map/all_to_all | solution.py:110
  135.6 7.0 %collective-permute-start.1 = (bf16[128,4,64]{0,2,1:T(8,128)(2,1)S(1)}, bf16[128,4,64]{0,2,1:T(8,128)(2,1)S(1)}, u32[]{:S(2)}, u32[]{:S(2)}) collective-permute-start(bf16[128,4,64]{0,2,1:T(8,128)(2,1)S(1)} %pad_maximum_fusion), channel_id=1, source_target_pairs={{0,4},{4,8},{8,12},{12,16},{16,20},{20,24},{24,28},{1,5},{5,9},{9,... | collective-permute-start | bytes 196616 | tf_op jit(solution)/shard_map/ppermute | solution.py:23
  139.1 5.6 %collective-permute-start = (bf16[128,4,64]{0,2,1:T(8,128)(2,1)S(1)}, bf16[128,4,64]{0,2,1:T(8,128)(2,1)S(1)}, u32[]{:S(2)}, u32[]{:S(2)}) collective-permute-start(bf16[128,4,64]{0,2,1:T(8,128)(2,1)S(1)} %bitcast.135), channel_id=1, source_target_pairs={{0,4},{4,8},{8,12},{12,16},{16,20},{20,24},{24,28},{1,5},{5,9},{9,... | collective-permute-start | bytes 196616 | tf_op jit(solution)/shard_map/ppermute | solution.py:23
  144.4 48.0 %copy-start.4 = (bf16[128,1440]{0,1:T(8,128)(2,1)S(1)}, bf16[128,1440]{0,1:T(8,128)(2,1)}, u32[]{:S(2)}) copy-start(bf16[128,1440]{0,1:T(8,128)(2,1)} %param.10) | copy-start | bytes 1105924
  192.4 5.4 %copy-start.6 = (f32[1440]{0:T(1024)S(1)}, f32[1440]{0:T(1024)}, u32[]{:S(2)}) copy-start(f32[1440]{0:T(1024)} %param.15) | copy-start | bytes 17284
  196.9 0.9 copy-start.2
  207.3 86.2 %slice-start = ((s8[4423680]{0:T(1024)(128)(4,1)}), s8[4194304]{0:T(1024)(128)(4,1)S(1)}, s32[]{:S(2)}) async-start(s8[4423680]{0:T(1024)(128)(4,1)} %bitcast.142), calls=%async_computation.5 | async-start | bytes 8388608
  278.6 15.0 %slice-start.1 = ((s8[4423680]{0:T(1024)(128)(4,1)}), s8[229376]{0:T(1024)(128)(4,1)S(1)}, s32[]{:S(2)}) async-start(s8[4423680]{0:T(1024)(128)(4,1)} %bitcast.142), calls=%async_computation.6 | async-start | bytes 458752
  305.1 4.9 %copy-start.5 = (s32[128,4]{0,1:T(4,128)S(1)}, s32[128,4]{0,1:T(4,128)}, u32[]{:S(2)}) copy-start(s32[128,4]{0,1:T(4,128)} %param.18) | copy-start | bytes 6148
  305.1 5.2 %copy-start.7 = (s32[128,4]{0,1:T(4,128)S(1)}, s32[128,4]{0,1:T(4,128)}, u32[]{:S(2)}) copy-start(s32[128,4]{0,1:T(4,128)} %param.19) | copy-start | bytes 6148
  305.1 70.1 %all-to-all-start.2 = ((bf16[8,128,1440]{1,2,0:T(8,128)(2,1)}), bf16[8,128,1440]{1,2,0:T(8,128)(2,1)}, u32[]{:S(2)}, u32[]{:S(2)}) async-start(bf16[8,128,1440]{1,2,0:T(8,128)(2,1)} %bitcast.124), calls=%async_computation.2 | async-start | bytes 5898240 | tf_op jit(solution)/shard_map/all_to_all | solution.py:146
  384.2 4.0 %copy-start.3 = (f32[128,1440]{0,1:T(8,128)S(1)}, f32[128,1440]{0,1:T(8,128)}, u32[]{:S(2)}) copy-start(f32[128,1440]{0,1:T(8,128)} %copy-done.2) | copy-start | bytes 2211844
  384.2 5.0 %copy-start.1 = (bf16[1440,320]{0,1:T(8,128)(2,1)S(1)}, bf16[1440,320]{0,1:T(8,128)(2,1)}, u32[]{:S(2)}) copy-start(bf16[1440,320]{0,1:T(8,128)(2,1)} %param.12) | copy-start | bytes 2764804
Sparse Core Ops, SparseCore 0:
  10.0 63.1 all-gather.2
  75.2 117.2 all-gather.4
where the time goes:
time: 397 us; the launch traced here: 396 us
  waiting for transfers between devices  227 us (57%)
  blocking collectives  71.3 us (18%)
  matrix products  33.8 us (9%)
  local copies, waits for them, and re-layouts  25.2 us (6%)
  between operations  13.8 us (3%)
  starting transfers between devices  13.6 us (3%)
  other arithmetic  11.8 us (3%)
    all_to_all x1, blocking collectives, local(): lax.all_to_all(outgoing, 'seq', split_axis=0, concat_axis=0, tiled=True)  71.3 us
    all_to_all x1, waiting for transfers between devices, local(): lax.all_to_all(run_expert(arrived, expert_in[0], expert_out[0]), 'seq', s...  64.8 us
    all_gather x1, waiting for transfers between devices, local(): lax.all_gather(normed, 'seq', axis=0, tiled=True)  59.4 us
    all_to_all x1, waiting for transfers between devices, local(): lax.all_to_all(spread, 'seq', split_axis=0, concat_axis=1, tiled=True)  53.5 us
    all_gather x1, waiting for transfers between devices, local(): lax.all_gather(out_weight, 'seq', axis=0, tiled=True)  46.5 us
    dot_general x1, matrix products, run_expert(): paired = jnp.dot(flat_rows, weight_in, preferred_element_type=jnp.float32)  15 us
    dot_general x1, matrix products, run_expert(): jnp.dot(activated, weight_out, preferred_element_type=jnp.float32)  9.39 us
    gather x3, local copies, waits for them, and re-layouts, local(): jnp.take(returned.reshape(-1, width), target, axis=0)  8.31 us
  transfers between devices with their start and end apart: 6, of which 6 were waited for; matrix products, arithmetic and copies ran while one was open for 3% of the time, Pallas kernels for 0%

commit v1 on v0

--- a/solution.py
+++ b/solution.py
@@ -1,8 +1,11 @@
+import functools
 import math
 
 import jax
 import jax.numpy as jnp
 from jax import lax
+from jax.experimental import pallas as pl
+from jax.experimental.pallas import tpu as pltpu
 from jax.sharding import PartitionSpec as P
 
 QH = 32
@@ -79,6 +82,162 @@
         jnp.bfloat16
     )
     return produced.reshape(incoming.shape)
+
+
+LANES = 128
+
+
+def ring_neighbours(axis, count):
+    index = lax.axis_index(axis)
+    row, column = index // 2, index % 2
+    rows = count // 2
+    up = column == 0
+    after = jnp.where(up, jnp.where(row < rows - 1, index + 2, index + 1), jnp.where(row > 0, index - 2, index - 1))
+    before = jnp.where(up, jnp.where(row > 0, index - 2, index + 1), jnp.where(row < rows - 1, index + 2, index - 1))
+    return after, before
+
+
+def greet(others, axis):
+    barrier = pltpu.get_barrier_semaphore()
+    for other in others:
+        pl.semaphore_signal(barrier, inc=1, device_id={axis: other}, device_id_type=pl.DeviceIdType.MESH)
+    pl.semaphore_wait(barrier, len(others))
+
+
+def moe_kernel(
+    count,
+    width,
+    x_ref,
+    residual_ref,
+    win_ref,
+    wout_ref,
+    out_ref,
+    rows_in,
+    part_out,
+    part_in,
+    own,
+    gather_send,
+    gather_recv,
+    part_send,
+    part_recv,
+):
+    half = x_ref.shape[0] // 2
+    hidden = wout_ref.shape[1]
+    me = lax.axis_index("seq")
+    targets = ring_neighbours("seq", count)
+    greet(targets, "seq")
+
+    def gather_copy(side, step, source):
+        return pltpu.make_async_remote_copy(
+            src_ref=source,
+            dst_ref=rows_in.at[step, side],
+            send_sem=gather_send.at[step, side],
+            recv_sem=gather_recv.at[step, side],
+            device_id={"seq": targets[side]},
+            device_id_type=pl.DeviceIdType.MESH,
+        )
+
+    def part_copy(side, step):
+        return pltpu.make_async_remote_copy(
+            src_ref=part_out.at[step, side],
+            dst_ref=part_in.at[step, side],
+            send_sem=part_send.at[step, side],
+            recv_sem=part_recv.at[step, side],
+            device_id={"seq": targets[side]},
+            device_id_type=pl.DeviceIdType.MESH,
+        )
+
+    def own_half(side):
+        return x_ref.at[pl.ds(side * half, half), :]
+
+    def expert(block):
+        paired = jnp.dot(block[:, :width], win_ref[0], preferred_element_type=jnp.float32)
+        gate_part = paired[:, :hidden]
+        up_part = paired[:, hidden:]
+        activated = gate_part * jax.nn.sigmoid(glu_slope * gate_part) * (up_part + 1.0)
+        produced = jnp.dot(
+            activated.astype(jnp.bfloat16), wout_ref[0], preferred_element_type=jnp.float32
+        )
+        tail = block[:, block.shape[1] - LANES :].astype(jnp.float32)
+        lane = lax.broadcasted_iota(jnp.int32, tail.shape, 1)
+        first = width - (block.shape[1] - LANES)
+        mine = (lane == first + me) | (lane == first + count + me)
+        weight = jnp.sum(jnp.where(mine, tail, 0.0), axis=1, keepdims=True)
+        return produced.astype(jnp.bfloat16).astype(jnp.float32) * weight
+
+    for side in range(2):
+        gather_copy(side, 1, own_half(side)).start()
+    own[...] = expert(x_ref[...]) + residual_ref[...].astype(jnp.float32)
+
+    def body(step, carry):
+        for side in range(2):
+            gather_copy(side, step, own_half(side)).wait_recv()
+
+        @pl.when(step < count - 1)
+        def _():
+            for side in range(2):
+                gather_copy(side, step + 1, rows_in.at[step, side]).start()
+
+        both = expert(rows_in[step].reshape(2 * half, rows_in.shape[-1]))
+
+        @pl.when(step > 1)
+        def _():
+            for side in range(2):
+                part_copy(side, step - 1).wait_recv()
+
+        for side in range(2):
+            before = part_in[step - 1, side].astype(jnp.float32)
+            before = jnp.where(step > 1, before, 0.0)
+            part_out[step, side] = (both[side * half : (side + 1) * half] + before).astype(jnp.bfloat16)
+            part_copy(side, step).start()
+        return carry
+
+    part_in[0] = jnp.zeros(part_in.shape[1:], part_in.dtype)
+    lax.fori_loop(1, count, body, 0)
+    for side in range(2):
+        part_copy(side, count - 1).wait_recv()
+        block = pl.ds(side * half, half)
+        out_ref[block, :] = (own[block, :] + part_in[count - 1, side].astype(jnp.float32)).astype(out_ref.dtype)
+
+    def drain(step, carry):
+        for side in range(2):
+            gather_copy(side, step, own_half(side)).wait_send()
+            part_copy(side, step).wait_send()
+        return carry
+
+    lax.fori_loop(1, count, drain, 0)
+
+
+def dense_experts(moe_input, residual_mid, route_weight, expert_ids, expert_in, expert_out):
+    rows, width = moe_input.shape
+    count = lax.axis_size("seq")
+    named = expert_ids[:, :, None] == jnp.arange(count)[None, None, :]
+    table = jnp.sum(jnp.where(named, route_weight[:, :, None], 0.0), axis=1)
+    high = lax.reduce_precision(table, 8, 7)
+    low = (table - high).astype(jnp.bfloat16)
+    padded = -(-(width + 2 * count) // LANES) * LANES
+    filler = jnp.zeros((rows, padded - width - 2 * count), jnp.bfloat16)
+    block = jnp.concatenate([moe_input, high.astype(jnp.bfloat16), low, filler], axis=1)
+    half = rows // 2
+    vmem = pl.BlockSpec(memory_space=pltpu.VMEM)
+    return pl.pallas_call(
+        functools.partial(moe_kernel, count, width),
+        out_shape=jax.ShapeDtypeStruct((rows, width), jnp.bfloat16),
+        in_specs=[vmem] * 4,
+        out_specs=vmem,
+        scratch_shapes=[
+            pltpu.VMEM((count, 2, half, padded), jnp.bfloat16),
+            pltpu.VMEM((count, 2, half, width), jnp.bfloat16),
+            pltpu.VMEM((count, 2, half, width), jnp.bfloat16),
+            pltpu.VMEM((rows, width), jnp.float32),
+            pltpu.SemaphoreType.DMA((count, 2)),
+            pltpu.SemaphoreType.DMA((count, 2)),
+            pltpu.SemaphoreType.DMA((count, 2)),
+            pltpu.SemaphoreType.DMA((count, 2)),
+        ],
+        compiler_params=pltpu.CompilerParams(collective_id=0, has_side_effects=True),
+        name="moe_ring",
+    )(block, residual_mid, expert_in, expert_out)
 
 
 def local(
@@ -107,7 +266,9 @@
         qkv_weight,
         preferred_element_type=jnp.float32,
     )
-    projections = lax.all_to_all(spread, "seq", split_axis=0, concat_axis=1, tiled=True)
+    projections = lax.all_to_all(
+        spread.astype(jnp.bfloat16), "seq", split_axis=0, concat_axis=1, tiled=True
+    ).astype(jnp.float32)
     first_pos = device_index * local_rows
     positions = (first_pos + jnp.arange(local_rows)).astype(jnp.float32)
     queries = rotate(projections[:, :query_cols].reshape(local_rows, QH, HD), positions).astype(
@@ -130,6 +291,13 @@
     )
     residual_mid = (residual + projected).astype(jnp.bfloat16)
     moe_input = norm_scale(residual_mid, moe_gain).astype(jnp.bfloat16)
+    route_weight = gate_ints.astype(jnp.float32)
+    route_weight = route_weight / jnp.sum(route_weight, axis=-1, keepdims=True)
+    tail = width % LANES + 2 * devices
+    if capacity >= local_rows and devices % 2 == 0 and tail <= LANES:
+        return dense_experts(
+            moe_input, residual_mid, route_weight, expert_ids, expert_in, expert_out
+        )
     flat_ids = expert_ids.reshape(-1)
     onehot = (flat_ids[:, None] == jnp.arange(devices)[None, :]).astype(jnp.int32)
     before = jnp.cumsum(onehot, axis=0) - onehot
@@ -151,8 +319,6 @@
         tiled=True,
     )
     picked = jnp.take(returned.reshape(-1, width), target, axis=0).reshape(local_rows, TOP, width)
-    route_weight = gate_ints.astype(jnp.float32)
-    route_weight = route_weight / jnp.sum(route_weight, axis=-1, keepdims=True)
     combined = residual_mid.astype(jnp.float32)
     for which in range(TOP):
         combined = combined + route_weight[:, which : which + 1] * picked[:, which].astype(

time: 397 us -> 268 us (0.68)
  waiting for transfers between devices: 227 us -> 155 us
  blocking collectives: 71.3 us -> 0 us
  Pallas kernels: 0 us -> 69.3 us
  matrix products: 33.8 us -> 9.64 us
  local copies, waits for them, and re-layouts: 25.2 us -> 5.54 us
  other arithmetic: 11.8 us -> 5.73 us
  starting transfers between devices: 13.6 us -> 8.07 us
    all_to_all x2 -> x1, waiting for transfers between devices: 118 us -> 31 us  [local(): lax.all_to_all(spread.astype(jnp.bfloat16), 'seq', split_axis=0, concat_a...]
    all_to_all x1 -> x0, blocking collectives: 71.3 us -> none  [local(): lax.all_to_all(outgoing, 'seq', split_axis=0, concat_axis=0, tiled=True)]
    pallas_call x0 -> x1, Pallas kernels: none -> 69.3 us  [dense_experts(): pl.pallas_call(functools.partial(moe_kernel, count, width), out_shape=jax...]
    dot_general x2 -> x0, matrix products: 24.4 us -> none  [the longest x1 15 us: run_expert(): paired = jnp.dot(flat_rows, weight_in, preferred_element_type=jnp.float32)]
    all_gather x1, waiting for transfers between devices: 46.5 us -> 63.4 us  [local(): lax.all_gather(out_weight, 'seq', axis=0, tiled=True)]
    gather x5 -> x0, local copies, waits for them, and re-layouts: 15.2 us -> none  [the longest x3 8.31 us: local(): jnp.take(returned.reshape(-1, width), target, axis=0)]
    all_to_all x2 -> x1, starting transfers between devices: 8.34 us -> 3.54 us  [local(): lax.all_to_all(spread.astype(jnp.bfloat16), 'seq', split_axis=0, concat_a...]
  transfers between devices with their start and end apart: 6 -> 5, of which waited for: 6 -> 4; matrix products, arithmetic and copies ran while one was open for 3% -> 4% of each run, Pallas kernels for 0% -> 0%
where the time goes in v1:
time: 268 us; the launch traced here: 267 us
  waiting for transfers between devices  155 us (58%)
  Pallas kernels  69.3 us (26%)
  between operations  13.6 us (5%)
  matrix products  9.64 us (4%)
  starting transfers between devices  8.07 us (3%)
  other arithmetic  5.73 us (2%)
  local copies, waits for them, and re-layouts  5.54 us (2%)
    pallas_call x1, Pallas kernels, dense_experts(): pl.pallas_call(functools.partial(moe_kernel, count, width), out_shape=jax...  69.3 us
    all_gather x1, waiting for transfers between devices, local(): lax.all_gather(out_weight, 'seq', axis=0, tiled=True)  63.4 us
    all_gather x1, waiting for transfers between devices, local(): lax.all_gather(normed, 'seq', axis=0, tiled=True)  60 us
    all_to_all x1, waiting for transfers between devices, local(): lax.all_to_all(spread.astype(jnp.bfloat16), 'seq', split_axis=0, concat_a...  31 us
  transfers between devices with their start and end apart: 5, of which 4 were waited for; matrix products, arithmetic and copies ran while one was open for 4% of the time, Pallas kernels for 0%

profile of v1, /device:TPU:0, one launch (start us, length us, event | category | flops | bytes accessed | tf_op | source)
XLA Modules:
  0.0 267.0 jit_solution(12620192521704312815)
XLA Ops:
  6.5 1.2 copy.31
  7.8 0.2 fusion.9
  8.0 1.7 fusion.11
  9.7 0.7 all-gather.5.cloned.1.call-update
  10.4 0.7 convert_reduce_fusion
  11.1 0.7 convert_divide_fusion
  11.8 0.7 select_reduce_fusion
  12.5 60.0 %all-gather.3.cloned.1.call-done = bf16[1024,1440]{1,0:T(8,128)(2,1)} async-done(((bf16[128,1440]{1,0:T(8,128)(2,1)}), bf16[1024,1440]{1,0:T(8,128)(2,1)}) %all-gather.3.cloned.1.call-update) | async-done | bytes 2949136 | tf_op jit(solution)/shard_map/all_gather | solution.py:265
  72.5 3.1 %fusion.5 = bf16[40,8,8,128]{3,2,1,0:T(8,128)(2,1)S(1)} fusion(bf16[1024,1440]{1,0:T(8,128)(2,1)} %all-gather.3.cloned.1.call-done, bf16[1440,320]{0,1:T(8,128)(2,1)S(1)} %copy-done), kind=kOutput, calls=%fused_computation.10 | convolution fusion | flops 944046080 | bytes 4526080 | tf_op jit(solution)/shard_map/dot_general | solution.py:264
  75.6 1.0 copy.45
  76.6 3.5 %all-to-all-start = ((bf16[8,128,320]{1,2,0:T(8,128)(2,1)}), bf16[8,128,320]{1,2,0:T(8,128)(2,1)S(1)}, u32[]{:S(2)}, u32[]{:S(2)}) async-start(bf16[8,128,320]{1,2,0:T(8,128)(2,1)} %bitcast.43), calls=%async_computation | async-start | bytes 1310720 | tf_op jit(solution)/shard_map/all_to_all | solution.py:269
  80.2 0.1 copy.35
  80.3 0.1 max.18
  80.4 0.1 copy.36
  80.5 0.1 copy.37
  80.7 0.1 multiply_cosine_fusion
  80.8 0.1 fusion.23
  81.0 31.0 %all-to-all-done = bf16[8,128,320]{1,2,0:T(8,128)(2,1)S(1)} async-done(((bf16[8,128,320]{1,2,0:T(8,128)(2,1)}), bf16[8,128,320]{1,2,0:T(8,128)(2,1)S(1)}, u32[]{:S(2)}, u32[]{:S(2)}) %all-to-all-start) | async-done | bytes 655392 | tf_op jit(solution)/shard_map/all_to_all | solution.py:269
  111.9 0.1 bitcast_convert_fusion
  112.2 2.6 collective-permute-start.1
  114.8 0.1 subtract_convert_fusion
  114.9 1.9 collective-permute-start
  116.9 0.8 fusion.1
  117.7 0.9 fusion
  118.6 0.1 exponential_add_fusion
  118.7 1.2 fusion.4
  119.9 63.4 %all-gather.5.cloned.1.call-done = bf16[2048,1440]{0,1:T(8,128)(2,1)} async-done(((bf16[256,1440]{0,1:T(8,128)(2,1)}), bf16[2048,1440]{0,1:T(8,128)(2,1)}) %all-gather.5.cloned.1.call-update) | async-done | bytes 5898256 | tf_op jit(solution)/shard_map/all_gather | solution.py:289
  183.3 4.6 %fusion.6 = (f32[128]{0:T(128)S(1)}, bf16[128,1440]{1,0:T(8,128)(2,1)S(1)}) fusion(bf16[128,2048]{0,1:T(8,128)(2,1)S(1)} %bitcast.46, bf16[2048,1440]{0,1:T(8,128)(2,1)} %all-gather.5.cloned.1.call-done, bf16[128,1440]{1,0:T(8,128)(2,1)S(1)} %copy.31), kind=kOutput, calls=%fused_computation.15 | convolution fusion | flops 756080512 | bytes 7160320 | tf_op jit(solution)/shard_map/dot_general | solution.py:287
  187.9 0.2 fusion.8
  188.1 0.9 concatenate.28.x_ref
  189.0 69.3 %moe_ring.1 = bf16[128,1440]{1,0:T(8,128)(2,1)} custom-call(bf16[128,1536]{1,0:T(8,128)(2,1)} %concatenate.28.x_ref, bf16[128,1440]{1,0:T(8,128)(2,1)} %copy-done.1, bf16[1,1440,2880]{2,1,0:T(8,128)(2,1)} %win_ref.1, bf16[1,1440,1440]{2,1,0:T(8,128)(2,1)} %wout_ref.1), custom_call_target="tpu_custom_call" | custom-call | tf_op jit(solution)/shard_map/moe_ring/pallas_call | solution.py:223
  258.3 1.9 copy.38
  (29 shorter events, 0.4 us)
Async XLA Ops:
  6.5 66.0 %copy-start = (bf16[1440,320]{0,1:T(8,128)(2,1)S(1)}, bf16[1440,320]{0,1:T(8,128)(2,1)}, u32[]{:S(2)}) copy-start(bf16[1440,320]{0,1:T(8,128)(2,1)} %param.12) | copy-start | bytes 2764804
  6.5 66.0 %all-gather.3.cloned.1.call-start = ((), (), s32[]{:S(2)}) async-start(), calls=%async_computation.1 | async-start | bytes 3538944 | tf_op jit(solution)/shard_map/all_gather | solution.py:265
  9.6 173.6 %all-gather.5.cloned.1.call-start = ((), (), s32[]{:S(2)}) async-start(), calls=%async_computation.2 | async-start | bytes 6635520 | tf_op jit(solution)/shard_map/all_gather | solution.py:289
  12.5 67.8 %copy-start.3 = (f32[32]{0:T(128)S(1)}, f32[32]{0:T(128)}, u32[]{:S(2)}) copy-start(f32[32]{0:T(128)} %param.13) | copy-start | bytes 388
  76.6 35.3 %all-to-all-start = ((bf16[8,128,320]{1,2,0:T(8,128)(2,1)}), bf16[8,128,320]{1,2,0:T(8,128)(2,1)S(1)}, u32[]{:S(2)}, u32[]{:S(2)}) async-start(bf16[8,128,320]{1,2,0:T(8,128)(2,1)} %bitcast.43), calls=%async_computation | async-start | bytes 1310720 | tf_op jit(solution)/shard_map/all_to_all | solution.py:269
  112.2 4.7 %collective-permute-start.1 = (bf16[128,4,64]{0,2,1:T(8,128)(2,1)S(1)}, bf16[128,4,64]{0,2,1:T(8,128)(2,1)S(1)}, u32[]{:S(2)}, u32[]{:S(2)}) collective-permute-start(bf16[128,4,64]{0,2,1:T(8,128)(2,1)S(1)} %pad_maximum_fusion), channel_id=1, source_target_pairs={{0,4},{4,8},{8,12},{12,16},{16,20},{20,24},{24,28},{1,5},{5,9},{9,... | collective-permute-start | bytes 196616 | tf_op jit(solution)/shard_map/ppermute | solution.py:26
  114.9 3.8 %collective-permute-start = (bf16[128,4,64]{0,2,1:T(8,128)(2,1)S(1)}, bf16[128,4,64]{0,2,1:T(8,128)(2,1)S(1)}, u32[]{:S(2)}, u32[]{:S(2)}) collective-permute-start(bf16[128,4,64]{0,2,1:T(8,128)(2,1)S(1)} %bitcast.50), channel_id=1, source_target_pairs={{0,4},{4,8},{8,12},{12,16},{16,20},{20,24},{24,28},{1,5},{5,9},{9,... | collective-permute-start | bytes 196616 | tf_op jit(solution)/shard_map/ppermute | solution.py:26
  119.9 68.0 %copy-start.2 = (f32[1440]{0:T(1024)S(1)}, f32[1440]{0:T(1024)}, u32[]{:S(2)}) copy-start(f32[1440]{0:T(1024)} %param.15) | copy-start | bytes 17284
  187.9 1.1 copy-start.1
Sparse Core Ops, SparseCore 0:
  9.8 62.7 all-gather.2
  74.6 108.6 all-gather.4

commit v2 on v1

--- a/solution.py
+++ b/solution.py
@@ -97,11 +97,12 @@
     return after, before
 
 
-def greet(others, axis):
+def greet(others, axis, more=()):
     barrier = pltpu.get_barrier_semaphore()
-    for other in others:
-        pl.semaphore_signal(barrier, inc=1, device_id={axis: other}, device_id_type=pl.DeviceIdType.MESH)
-    pl.semaphore_wait(barrier, len(others))
+    devices = [{axis: other} for other in others] + list(more)
+    for device in devices:
+        pl.semaphore_signal(barrier, inc=1, device_id=device, device_id_type=pl.DeviceIdType.MESH)
+    pl.semaphore_wait(barrier, len(devices))
 
 
 def moe_kernel(
@@ -240,6 +241,162 @@
     )(block, residual_mid, expert_in, expert_out)
 
 
+def weights_kernel(
+    count,
+    x_ref,
+    qkv_ref,
+    out_weight_ref,
+    spread_ref,
+    out_all_ref,
+    qkv_all,
+    ring_send,
+    ring_recv,
+    across_send,
+    across_recv,
+    core_send,
+    core_recv,
+):
+    me = lax.axis_index("seq")
+    seat = lax.axis_index("batch")
+    core, side = seat % 2, seat // 2
+    partner, across = seat + 1 - 2 * core, seat + 2 - 4 * side
+    rows = count // 2
+    place = jnp.where(me % 2 == 0, me // 2, count - 1 - me // 2)
+    targets = ring_neighbours("seq", count)
+    greet(targets, "seq", ({"batch": partner}, {"batch": across}))
+    shards = (qkv_ref, out_weight_ref)
+    gathered = (qkv_all, out_all_ref)
+
+    def shard_at(position):
+        position = lax.rem(position + count, count)
+        return jnp.where(position < rows, 2 * position, 2 * (count - 1 - position) + 1)
+
+    def piece(which, third):
+        size = shards[which].shape[0] // 6
+        return pl.ds(pl.multiple_of((third * 2 + core) * size, 16), size)
+
+    def remote(source, target, send, recv, device):
+        return pltpu.make_async_remote_copy(
+            src_ref=source,
+            dst_ref=target,
+            send_sem=send,
+            recv_sem=recv,
+            device_id=device,
+            device_id_type=pl.DeviceIdType.MESH,
+        )
+
+    def ring_copy(way, step, which, first=False):
+        shard = shard_at(place + (1 - 2 * way) * (1 - step))
+        span = piece(which, side + way)
+        target = gathered[which].at[shard, span]
+        source = shards[which].at[span] if first else target
+        sems = ring_send.at[way, step, which], ring_recv.at[way, step, which]
+        return remote(source, target, *sems, {"seq": targets[way]})
+
+    def across_copy(step, which):
+        shard = shard_at(place + (2 * side - 1) * step)
+        target = gathered[which].at[shard, piece(which, 2 * side)]
+        sems = across_send.at[step, which], across_recv.at[step, which]
+        return remote(target, target, *sems, {"batch": across})
+
+    def core_copy(kind, step, which):
+        third = (side, side + 1, 2 * (1 - side))[kind]
+        offset = (-step, step, (1 - 2 * side) * step)[kind]
+        target = gathered[which].at[shard_at(place + offset), piece(which, third)]
+        sems = core_send.at[kind, step, which], core_recv.at[kind, step, which]
+        return remote(target, target, *sems, {"batch": partner})
+
+    for which in range(2):
+        for way in range(2):
+            ring_copy(way, 1, which, True).start()
+    for which in range(2):
+        gathered[which][me] = shards[which][...]
+
+    def body(step, carry):
+        for which in range(2):
+            for way in range(2):
+                ring_copy(way, step, which).wait_recv()
+
+                @pl.when(step < count - 1)
+                def _():
+                    ring_copy(way, step + 1, which).start()
+
+            across_copy(step, which).start()
+            for way in range(2):
+                core_copy(way, step, which).start()
+
+            @pl.when(step > 1)
+            def _():
+                across_copy(step - 1, which).wait_recv()
+                core_copy(2, step - 1, which).start()
+
+        return carry
+
+    lax.fori_loop(1, count, body, 0)
+    for which in range(2):
+        across_copy(count - 1, which).wait_recv()
+        core_copy(2, count - 1, which).start()
+
+    def arrived(which):
+        def wait(step, carry):
+            for kind in range(3):
+                core_copy(kind, step, which).wait_recv()
+            return carry
+
+        lax.fori_loop(1, count, wait, 0)
+
+    arrived(0)
+
+    def project(shard, carry):
+        spread_ref[shard] = jnp.dot(x_ref[...], qkv_all[shard], preferred_element_type=jnp.float32)
+        return carry
+
+    lax.fori_loop(0, count, project, 0)
+    arrived(1)
+
+    def drain(step, carry):
+        for which in range(2):
+            for way in range(2):
+                ring_copy(way, step, which).wait_send()
+            across_copy(step, which).wait_send()
+            for kind in range(3):
+                core_copy(kind, step, which).wait_send()
+        return carry
+
+    lax.fori_loop(1, count, drain, 0)
+
+
+def gather_weights(normed, qkv_weight, out_weight):
+    count = lax.axis_size("seq")
+    depth = out_weight.shape[0]
+    padded = -(-depth // 96) * 96
+    out_weight = jnp.pad(out_weight, ((0, padded - depth), (0, 0)))
+    vmem = pl.BlockSpec(memory_space=pltpu.VMEM)
+    shape = (normed.shape[0], qkv_weight.shape[1])
+    dma = pltpu.SemaphoreType.DMA
+    spread, out_all = pl.pallas_call(
+        functools.partial(weights_kernel, count),
+        out_shape=(
+            jax.ShapeDtypeStruct((count, *shape), jnp.float32),
+            jax.ShapeDtypeStruct((count, *out_weight.shape), jnp.bfloat16),
+        ),
+        in_specs=[vmem] * 3,
+        out_specs=(vmem, vmem),
+        scratch_shapes=[
+            pltpu.VMEM((count, *qkv_weight.shape), jnp.bfloat16),
+            dma((2, count, 2)),
+            dma((2, count, 2)),
+            dma((count, 2)),
+            dma((count, 2)),
+            dma((3, count, 2)),
+            dma((3, count, 2)),
+        ],
+        compiler_params=pltpu.CompilerParams(collective_id=1, has_side_effects=True),
+        name="weights_ring",
+    )(normed, qkv_weight, out_weight)
+    return spread, out_all.reshape(count * padded, -1), padded
+
+
 def local(
     tokens,
     norm_gain,
@@ -261,14 +418,21 @@
     key_cols = KVH * HD
     residual = tokens.astype(jnp.float32)
     normed = norm_scale(tokens, norm_gain).astype(jnp.bfloat16)
-    spread = jnp.dot(
-        lax.all_gather(normed, "seq", axis=0, tiled=True),
-        qkv_weight,
-        preferred_element_type=jnp.float32,
-    )
-    projections = lax.all_to_all(
-        spread.astype(jnp.bfloat16), "seq", split_axis=0, concat_axis=1, tiled=True
-    ).astype(jnp.float32)
+    tail = width % LANES + 2 * devices
+    dense = capacity >= local_rows and devices % 2 == 0 and tail <= LANES
+    shared = dense and lax.axis_size("batch") == 4 and width % 96 == 0
+    if shared:
+        spread, out_all, padded = gather_weights(normed, qkv_weight, out_weight)
+        projections = spread.transpose(1, 0, 2).reshape(local_rows, -1)
+    else:
+        spread = jnp.dot(
+            lax.all_gather(normed, "seq", axis=0, tiled=True),
+            qkv_weight,
+            preferred_element_type=jnp.float32,
+        )
+        projections = lax.all_to_all(
+            spread.astype(jnp.bfloat16), "seq", split_axis=0, concat_axis=1, tiled=True
+        ).astype(jnp.float32)
     first_pos = device_index * local_rows
     positions = (first_pos + jnp.arange(local_rows)).astype(jnp.float32)
     queries = rotate(projections[:, :query_cols].reshape(local_rows, QH, HD), positions).astype(
@@ -284,17 +448,23 @@
     key_block = jnp.concatenate([prev_keys, key_heads], axis=0)
     value_block = jnp.concatenate([prev_values, value_heads], axis=0)
     attention = band_block(queries, key_block, value_block, sinks, first_pos)
-    projected = jnp.dot(
-        attention,
-        lax.all_gather(out_weight, "seq", axis=0, tiled=True),
-        preferred_element_type=jnp.float32,
-    )
+    if shared:
+        depth = query_cols // devices
+        spaced = jnp.pad(
+            attention.reshape(local_rows, devices, depth), ((0, 0), (0, 0), (0, padded - depth))
+        ).reshape(local_rows, devices * padded)
+        projected = jnp.dot(spaced, out_all, preferred_element_type=jnp.float32)
+    else:
+        projected = jnp.dot(
+            attention,
+            lax.all_gather(out_weight, "seq", axis=0, tiled=True),
+            preferred_element_type=jnp.float32,
+        )
     residual_mid = (residual + projected).astype(jnp.bfloat16)
     moe_input = norm_scale(residual_mid, moe_gain).astype(jnp.bfloat16)
     route_weight = gate_ints.astype(jnp.float32)
     route_weight = route_weight / jnp.sum(route_weight, axis=-1, keepdims=True)
-    tail = width % LANES + 2 * devices
-    if capacity >= local_rows and devices % 2 == 0 and tail <= LANES:
+    if dense:
         return dense_experts(
             moe_input, residual_mid, route_weight, expert_ids, expert_in, expert_out
         )

time: 268 us -> 170 us (0.63)
  waiting for transfers between devices: 155 us -> 0.98 us
  Pallas kernels: 69.3 us -> 143 us
  between operations: 13.6 us -> 0.28 us
  local copies, waits for them, and re-layouts: 5.54 us -> 12.9 us
  matrix products: 9.64 us -> 3.15 us
  other arithmetic: 5.73 us -> 2.83 us
    all_gather x2 -> x0, waiting for transfers between devices: 123 us -> none  [the longest x1 63.4 us: local(): lax.all_gather(out_weight, 'seq', axis=0, tiled=True)]
    pallas_call x0 -> x1, Pallas kernels: none -> 70.9 us  [gather_weights(): pl.pallas_call(functools.partial(weights_kernel, count), out_shape=(jax.S...]
    all_to_all x1 -> x0, waiting for transfers between devices: 31 us -> none  [local(): lax.all_to_all(spread.astype(jnp.bfloat16), 'seq', split_axis=0, concat_a...]
    dot_general x2 -> x1, matrix products: 7.72 us -> 1.23 us  [local(): projected = jnp.dot(spaced, out_all, preferred_element_type=jnp.float32)]
    unnamed x9 -> x19, local copies, waits for them, and re-layouts: 1.26 us -> 6.79 us
    all_to_all x1 -> x0, starting transfers between devices: 3.54 us -> none  [local(): lax.all_to_all(spread.astype(jnp.bfloat16), 'seq', split_axis=0, concat_a...]
  transfers between devices with their start and end apart: 5 -> 2, of which waited for: 4 -> 1; matrix products, arithmetic and copies ran while one was open for 4% -> 2% of each run, Pallas kernels for 0% -> 0%
where the time goes in v2:
time: 170 us
  Pallas kernels  143 us (84%)
  local copies, waits for them, and re-layouts  12.9 us (8%)
  starting transfers between devices  6.85 us (4%)
  matrix products  3.15 us (2%)
  other arithmetic  2.83 us (2%)
    pallas_call x1, Pallas kernels, dense_experts(): pl.pallas_call(functools.partial(moe_kernel, count, width), out_shape=jax...  71.7 us
    pallas_call x1, Pallas kernels, gather_weights(): pl.pallas_call(functools.partial(weights_kernel, count), out_shape=(jax.S...  70.9 us
    ppermute x2, starting transfers between devices, shifted(): lax.ppermute(value, axis, [(source, source + steps) for source in range(i...  6.85 us
    unnamed x19, local copies, waits for them, and re-layouts  6.79 us
  transfers between devices with their start and end apart: 2, of which 1 were waited for; matrix products, arithmetic and copies ran while one was open for 2% of the time, Pallas kernels for 0%

profile of v2, /device:TPU:0, one launch (start us, length us, event | category | flops | bytes accessed | tf_op | source)
XLA Modules:
  0.0 169.6 jit_solution(440012475419494451)
XLA Ops:
  0.0 1.2 copy.37
  1.2 0.2 fusion.9
  1.4 1.4 copy.38
  2.8 2.4 %copy.39.qkv_ref = bf16[1440,320]{1,0:T(8,128)(2,1)} copy(bf16[1440,320]{0,1:T(8,128)(2,1)} %param.12) | data formatting | bytes 1843200 | tf_op args[2]
  5.1 0.9 fusion.11.x_ref
  6.1 1.0 pad.8.out_weight_ref
  7.0 70.9 %weights_ring.1 = (f32[8,128,320]{2,1,0:T(8,128)}, bf16[8,288,1440]{2,1,0:T(8,128)(2,1)}) custom-call(bf16[128,1440]{1,0:T(8,128)(2,1)} %fusion.11.x_ref, bf16[1440,320]{1,0:T(8,128)(2,1)} %copy.39.qkv_ref, bf16[288,1440]{1,0:T(8,128)(2,1)} %pad.8.out_weight_ref), custom_call_target="tpu_custom_call" | custom-call | tf_op jit(solution)/shard_map/weights_ring/pallas_call | solution.py:377
  77.9 0.0 copy-start.5
  77.9 1.9 %copy.40 = f32[128,8,320]{0,2,1:T(8,128)S(1)} copy(f32[128,8,320]{2,0,1:T(8,128)} %bitcast.46) | data formatting | bytes 2621440 | tf_op jit(solution)/shard_map/transpose | solution.py:426
  79.8 3.4 %collective-permute-start = (bf16[128,4,64]{0,2,1:T(8,128)(2,1)S(1)}, bf16[128,4,64]{0,2,1:T(8,128)(2,1)S(1)}, u32[]{:S(2)}, u32[]{:S(2)}) collective-permute-start(bf16[128,4,64]{0,2,1:T(8,128)(2,1)S(1)} %bitcast.51), channel_id=1, source_target_pairs={{0,4},{4,8},{8,12},{12,16},{16,20},{20,24},{24,28},{1,5},{5,9},{9,... | collective-permute-start | bytes 196616 | tf_op jit(solution)/shard_map/ppermute | solution.py:26
  83.3 0.1 multiply_cosine_fusion
  83.5 3.4 %collective-permute-start.1 = (bf16[128,4,64]{0,2,1:T(8,128)(2,1)S(1)}, bf16[128,4,64]{0,2,1:T(8,128)(2,1)S(1)}, u32[]{:S(2)}, u32[]{:S(2)}) collective-permute-start(bf16[128,4,64]{0,2,1:T(8,128)(2,1)S(1)} %pad_maximum_fusion), channel_id=1, source_target_pairs={{0,4},{4,8},{8,12},{12,16},{16,20},{20,24},{24,28},{1,5},{5,9},{9,... | collective-permute-start | bytes 196616 | tf_op jit(solution)/shard_map/ppermute | solution.py:26
  87.0 0.1 copy.43
  87.1 0.1 slice.33
  87.2 0.1 copy.44
  87.3 0.1 subtract_convert_fusion
  87.5 0.1 fusion.24
  87.6 0.1 max.18
  87.7 0.1 copy.45
  87.8 1.0 collective-permute-done.1
  88.8 0.8 fusion.1
  89.6 0.1 broadcast_maximum_fusion
  89.6 0.9 fusion
  90.5 0.1 exponential_add_fusion
  90.6 1.2 fusion.5
  91.8 0.9 slice-done
  92.7 0.9 slice-done.1
  93.6 1.2 fusion.6
  94.9 0.2 fusion.8
  95.1 0.9 concatenate.28.x_ref
  95.9 71.7 %moe_ring.1 = bf16[128,1440]{1,0:T(8,128)(2,1)} custom-call(bf16[128,1536]{1,0:T(8,128)(2,1)} %concatenate.28.x_ref, bf16[128,1440]{1,0:T(8,128)(2,1)} %copy-done, bf16[1,1440,2880]{2,1,0:T(8,128)(2,1)} %win_ref.1, bf16[1,1440,1440]{2,1,0:T(8,128)(2,1)} %wout_ref.1), custom_call_target="tpu_custom_call" | custom-call | tf_op jit(solution)/shard_map/moe_ring/pallas_call | solution.py:224
  167.7 1.9 %copy.46 = bf16[128,1440]{0,1:T(8,128)(2,1)} copy(bf16[128,1440]{1,0:T(8,128)(2,1)} %moe_ring.1) | data formatting | bytes 737280 | tf_op jit(solution)/shard_map/moe_ring/pallas_call | solution.py:224
  (32 shorter events, 0.2 us)
Async XLA Ops:
  0.0 5.1 %copy-start.1 = (f32[1440]{0:T(1024)S(1)}, f32[1440]{0:T(1024)}, u32[]{:S(2)}) copy-start(f32[1440]{0:T(1024)} %param.11) | copy-start | bytes 17284
  5.1 81.8 %copy-start.3 = (s32[128,4]{0,1:T(4,128)S(1)}, s32[128,4]{0,1:T(4,128)}, u32[]{:S(2)}) copy-start(s32[128,4]{0,1:T(4,128)} %param.19) | copy-start | bytes 6148
  5.1 81.9 %copy-start.4 = (s32[128,4]{0,1:T(4,128)S(1)}, s32[128,4]{0,1:T(4,128)}, u32[]{:S(2)}) copy-start(s32[128,4]{0,1:T(4,128)} %param.18) | copy-start | bytes 6148
  77.9 9.7 %copy-start.5 = (f32[32]{0:T(128)S(1)}, f32[32]{0:T(128)}, u32[]{:S(2)}) copy-start(f32[32]{0:T(128)} %param.13) | copy-start | bytes 388
  79.8 10.8 %collective-permute-start = (bf16[128,4,64]{0,2,1:T(8,128)(2,1)S(1)}, bf16[128,4,64]{0,2,1:T(8,128)(2,1)S(1)}, u32[]{:S(2)}, u32[]{:S(2)}) collective-permute-start(bf16[128,4,64]{0,2,1:T(8,128)(2,1)S(1)} %bitcast.51), channel_id=1, source_target_pairs={{0,4},{4,8},{8,12},{12,16},{16,20},{20,24},{24,28},{1,5},{5,9},{9,... | collective-permute-start | bytes 196616 | tf_op jit(solution)/shard_map/ppermute | solution.py:26
  83.5 5.3 %collective-permute-start.1 = (bf16[128,4,64]{0,2,1:T(8,128)(2,1)S(1)}, bf16[128,4,64]{0,2,1:T(8,128)(2,1)S(1)}, u32[]{:S(2)}, u32[]{:S(2)}) collective-permute-start(bf16[128,4,64]{0,2,1:T(8,128)(2,1)S(1)} %pad_maximum_fusion), channel_id=1, source_target_pairs={{0,4},{4,8},{8,12},{12,16},{16,20},{20,24},{24,28},{1,5},{5,9},{9,... | collective-permute-start | bytes 196616 | tf_op jit(solution)/shard_map/ppermute | solution.py:26
  90.5 2.2 %slice-start = ((s8[7077888]{0:T(1024)(128)(4,1)}), s8[4194304]{0:T(1024)(128)(4,1)S(1)}, s32[]{:S(2)}) async-start(s8[7077888]{0:T(1024)(128)(4,1)} %bitcast.40), calls=%async_computation | async-start | bytes 8388608
  90.6 3.0 %slice-start.1 = ((s8[7077888]{0:T(1024)(128)(4,1)}), s8[2883584]{0:T(1024)(128)(4,1)S(1)}, s32[]{:S(2)}) async-start(s8[7077888]{0:T(1024)(128)(4,1)} %bitcast.40), calls=%async_computation.1 | async-start | bytes 5767168
  93.6 1.3 copy-start.2
  94.9 1.1 copy-start
